TPU v7x, 32 devices: a whole 2x2x4 slice. The times are simulated.
32 devices in a mesh: ep: 8 (over z, x), tp: 4 (over y, core).
Axes of the slice: x: 2, y: 2, z: 4, core: 2. Of those that a mesh axis runs over, the one named last changes fastest.
Arguments:
- hidden: bfloat16 [512, 2880], P('ep'), may hold values from -0.59765625 to 0.59765625
- queries: bfloat16 [512, 2048], P('ep', 'tp'), may hold values from -160 to 160
- new_keys: bfloat16 [512, 256], P('ep', 'tp'), may hold values from -6 to 6
- new_values: bfloat16 [512, 256], P('ep', 'tp'), may hold values from -6 to 6
- key_cache: bfloat16 [64, 4, 64, 1024], P('ep', 'tp'), may hold values from -6 to 6
- value_cache: bfloat16 [64, 4, 64, 1024], P('ep', 'tp'), may hold values from -6 to 6
- cache_lengths: int32 [64], P('ep'), may hold values from 16 to 1024
- w_out: bfloat16 [2048, 2880], P('tp'), may hold values from -0.125 to 0.125
- w_router: bfloat16 [2880, 8], replicated, may hold values from -0.109375 to 0.109375
- routes: int32 [512, 4], P('ep'), may hold values from 0 to 7, all different within a row; in each aligned block of 16 rows (0 to 15, 16 to 31, ...) at most 16 rows name the same one
- w_gate: bfloat16 [8, 2880, 1536], P('ep', None, 'tp'), may hold values from -0.109375 to 0.109375
- w_up: bfloat16 [8, 2880, 1536], P('ep', None, 'tp'), may hold values from -0.109375 to 0.109375
- w_down: bfloat16 [8, 1536, 2880], P('ep', 'tp'), may hold values from -0.15625 to 0.15625
Outputs:
- layer_out: bfloat16 [512, 2880], P(('ep', 'tp'))
Inputs may be any that keep to these rules, and one draw needn't show every extreme that they name: `routes`: each token names 4 different experts; in each aligned block of 16 tokens no expert is named by more than 16 tokens, and in some blocks one expert is named by exactly 16.
All inputs are finite; a program needn't handle non-finite values.
Results may differ from a plain program's by a relative error of at most 0.02.
Values may be sent and summed in bfloat16 or wider, within the bound.
A program may use at most 64 MiB of HBM per device.

v0:
```python
import jax
import jax.numpy as jnp
from jax import lax
from jax.sharding import PartitionSpec as P


def attend(queries, new_keys, new_values, key_cache, value_cache, cache_lengths):
    seq_count, kv_count, head_dim, length = key_cache.shape
    new_count = queries.shape[0] // seq_count
    group_size = queries.shape[1] // (kv_count * head_dim)
    row_count = new_count * group_size
    scale = head_dim ** (-0.5)
    query_block = queries.reshape(seq_count, new_count, kv_count, group_size, head_dim)
    query_block = query_block.transpose(0, 2, 1, 3, 4).reshape(
        seq_count, kv_count, row_count, head_dim
    )
    fresh_keys = new_keys.reshape(seq_count, new_count, kv_count, head_dim).transpose(0, 2, 1, 3)
    fresh_values = new_values.reshape(seq_count, new_count, kv_count, head_dim).transpose(
        0, 2, 1, 3
    )
    cache_scores = (
        jnp.einsum("skrd,skdl->skrl", query_block, key_cache, preferred_element_type=jnp.float32)
        * scale
    )
    in_cache = jnp.arange(length)[None, :] < cache_lengths[:, None]
    cache_scores = jnp.where(in_cache[:, None, None, :], cache_scores, -1e30)
    fresh_scores = (
        jnp.einsum("skrd,sknd->skrn", query_block, fresh_keys, preferred_element_type=jnp.float32)
        * scale
    )
    causal = (jnp.arange(row_count) // group_size)[:, None] >= jnp.arange(new_count)[None, :]
    fresh_scores = jnp.where(causal[None, None, :, :], fresh_scores, -1e30)
    row_max = jnp.maximum(
        jnp.max(cache_scores, -1, keepdims=True), jnp.max(fresh_scores, -1, keepdims=True)
    )
    cache_exp = jnp.exp(cache_scores - row_max)
    fresh_exp = jnp.exp(fresh_scores - row_max)
    denom_sum = jnp.sum(cache_exp, -1, keepdims=True) + jnp.sum(fresh_exp, -1, keepdims=True)
    cache_probs = (cache_exp / denom_sum).astype(jnp.bfloat16)
    fresh_probs = (fresh_exp / denom_sum).astype(jnp.bfloat16)
    head_mix = jnp.einsum(
        "skrl,skdl->skrd", cache_probs, value_cache, preferred_element_type=jnp.float32
    )
    head_mix = head_mix + jnp.einsum(
        "skrn,sknd->skrd", fresh_probs, fresh_values, preferred_element_type=jnp.float32
    )
    head_mix = head_mix.reshape(seq_count, kv_count, new_count, group_size, head_dim).transpose(
        0, 2, 1, 3, 4
    )
    return head_mix.reshape(seq_count * new_count, kv_count * group_size * head_dim).astype(
        jnp.bfloat16
    )


def expert_apply(received, w_gate, w_up, w_down):
    width = received.shape[-1]
    flat_rows = received.reshape(-1, width)
    gate_proj = jnp.dot(flat_rows, w_gate[0], preferred_element_type=jnp.float32)
    up_proj = jnp.dot(flat_rows, w_up[0], preferred_element_type=jnp.float32)
    activated = ((up_proj + 1.0) * gate_proj * jax.nn.sigmoid(1.702 * gate_proj)).astype(
        jnp.bfloat16
    )
    partial_out = jnp.dot(activated, w_down[0], preferred_element_type=jnp.float32)
    return partial_out.reshape(received.shape[0], received.shape[1], width)


def body(
    hidden,
    queries,
    new_keys,
    new_values,
    key_cache,
    value_cache,
    cache_lengths,
    w_out,
    w_router,
    routes,
    w_gate,
    w_up,
    w_down,
):
    tp_size = lax.axis_size("tp")
    tp_index = lax.axis_index("tp")
    width = hidden.shape[1]
    block_rows = hidden.shape[0] // tp_size
    top_count = routes.shape[1]
    experts = w_router.shape[1]
    capacity = min(block_rows, max(2, (2 * block_rows * top_count + experts - 1) // experts))
    start_row = tp_index * block_rows
    attended = attend(queries, new_keys, new_values, key_cache, value_cache, cache_lengths)
    partial_value = jnp.dot(attended, w_out, preferred_element_type=jnp.float32)
    summed = lax.psum_scatter(
        partial_value.astype(jnp.bfloat16), "tp", scatter_dimension=0, tiled=True
    ).astype(jnp.float32)
    residual = (
        lax.dynamic_slice_in_dim(hidden, start_row, block_rows, 0).astype(jnp.float32) + summed
    )
    local_routes = lax.dynamic_slice_in_dim(routes, start_row, block_rows, 0)
    block_count = 1
    normed = (
        residual * lax.rsqrt(jnp.mean(residual * residual, -1, keepdims=True) + 1e-05)
    ).astype(jnp.bfloat16)
    logits = jnp.dot(normed, w_router, preferred_element_type=jnp.float32)
    expert_ids = jnp.arange(experts, dtype=jnp.int32)
    matches = local_routes[:, :, None] == expert_ids[None, None, :]
    picked = jnp.sum(jnp.where(matches, logits[:, None, :], 0.0), -1)
    picked_exp = jnp.exp(picked)
    weights = picked_exp / jnp.sum(picked_exp, -1, keepdims=True)
    flat_routes = local_routes.reshape(-1)
    one_hot = (
        flat_routes.reshape(block_count, block_rows * top_count)[:, :, None]
        == expert_ids[None, None, :]
    ).astype(jnp.int32)
    slot_rank = jnp.sum((jnp.cumsum(one_hot, 1) - one_hot) * one_hot, -1)
    slot_index = (
        slot_rank + (jnp.arange(block_count, dtype=jnp.int32) * capacity)[:, None]
    ).reshape(-1)
    outgoing = jnp.zeros((experts, block_count * capacity, width), jnp.bfloat16)
    outgoing = outgoing.at[flat_routes, slot_index].set(jnp.repeat(normed, top_count, axis=0))
    grouped = expert_apply(
        lax.all_gather(
            lax.all_to_all(outgoing, "ep", split_axis=0, concat_axis=0, tiled=True),
            "tp",
            axis=1,
            tiled=True,
        ),
        w_gate,
        w_up,
        w_down,
    )
    group_total = lax.psum_scatter(
        grouped.astype(jnp.bfloat16), "tp", scatter_dimension=1, tiled=True
    ).astype(jnp.float32)
    returned = lax.all_to_all(
        group_total.astype(jnp.bfloat16), "ep", split_axis=0, concat_axis=0, tiled=True
    ).astype(group_total.dtype)
    routed = returned[flat_routes, slot_index].reshape(-1, top_count, width)
    mixture = jnp.sum(weights[:, :, None] * routed, 1)
    return (residual + mixture).astype(jnp.bfloat16)


def solution(mesh):
    return jax.shard_map(
        body,
        mesh=mesh,
        in_specs=(
            P("ep", None),
            P("ep", "tp"),
            P("ep", "tp"),
            P("ep", "tp"),
            P("ep", "tp", None, None),
            P("ep", "tp", None, None),
            P("ep"),
            P("tp", None),
            P(),
            P("ep", None),
            P("ep", None, "tp"),
            P("ep", None, "tp"),
            P("ep", "tp", None),
        ),
        out_specs=P(("ep", "tp"), None),
        check_vma=False,
    )
```

profile of v0, /device:TPU:0, one launch (start us, length us, event | category | flops | bytes accessed | tf_op | source)
XLA Modules:
  0.0 197.5 jit_solution(2319943355972274330)
XLA Ops:
  6.6 0.9 iota_compare_fusion.1
  7.4 1.0 reshape.298
  8.4 0.9 fusion.37
  9.3 0.0 copy-start.8
  9.3 1.8 fusion.5
  11.2 0.6 fusion.6
  11.9 0.0 copy-done.8
  11.9 0.0 copy-start.3
  11.9 0.7 fusion.21
  12.6 0.2 fusion.19
  12.9 0.0 copy-start.4
  12.9 0.1 convert_element_type.59
  13.1 1.7 convolution_convert_fusion.1
  14.8 0.0 reduce-scatter.3.cloned.1.call-update
  14.8 0.0 all-gather.2.cloned.1.call-start
  14.9 0.1 constant_dynamic-slice_fusion
  15.0 0.1 copy.23
  15.1 0.1 eq.43
  15.1 0.1 reshape.303
  15.2 0.1 fusion.26
  15.3 0.1 reduce_window_sum.11
  15.4 0.2 select_reduce_fusion
  15.6 22.9 %reduce-scatter.3.cloned.1.call-done = bf16[16,2880]{1,0:T(8,128)(2,1)} async-done(((bf16[64,2880]{1,0:T(8,128)(2,1)}), bf16[16,2880]{1,0:T(8,128)(2,1)}) %reduce-scatter.3.cloned.1.call-update) | async-done | bytes 92176 | tf_op jit(solution)/shard_map/reduce_scatter | solution.py:92
  38.5 1.1 multiply_reduce_fusion.1
  39.5 1.0 multiply_convert_fusion
  40.6 0.8 broadcast_in_dim.70
  41.4 1.2 reshape.315
  42.6 0.9 broadcast_in_dim.46
  43.5 13.9 %scatter_fusion = bf16[8,16,2880]{2,1,0:T(8,128)(2,1)} fusion(bf16[8,16,2880]{2,1,0:T(8,128)(2,1)} %broadcast_in_dim.46, s32[64]{0:T(128)S(1)} %get-tuple-element.5, bf16[64,2880]{1,0:T(8,128)(2,1)S(1)} %reshape.315), kind=kCustom, calls=%fused_computation.1 | custom fusion | bytes 1106432 | tf_op jit(solution)/shard_map/scatter | solution.py:119
  57.4 24.7 %all_to_all.10 = bf16[8,16,2880]{2,1,0:T(8,128)(2,1)} all-to-all(bf16[8,16,2880]{2,1,0:T(8,128)(2,1)} %scatter_fusion), channel_id=1, replica_groups=mesh['ep'=8,'tp'=4] {'ep'}, dimensions={0} | all-to-all | bytes 1474560 | tf_op jit(solution)/shard_map/all_to_all | solution.py:122
  82.1 0.0 all-gather.2.cloned.1.call-update
  82.2 0.0 reduce-scatter.5.cloned.1.call-start
  82.2 26.1 %all-gather.2.cloned.1.call-done = bf16[8,64,2880]{2,1,0:T(8,128)(2,1)} async-done(((bf16[8,16,2880]{2,1,0:T(8,128)(2,1)}), bf16[8,64,2880]{2,1,0:T(8,128)(2,1)}) %all-gather.2.cloned.1.call-update) | async-done | bytes 2949136 | tf_op jit(solution)/shard_map/all_gather | solution.py:121
  108.3 4.4 %fusion.1 = f32[512,384]{1,0:T(8,128)S(1)} fusion(bf16[512,2880]{1,0:T(8,128)(2,1)} %bitcast.57, bf16[1,2880,384]{2,1,0:T(8,128)(2,1)} %param.23), kind=kOutput, calls=%fused_computation.5 | convolution fusion | flops 1132462080 | bytes 5947392 | tf_op jit(solution)/shard_map/dot_general | solution.py:58
  112.7 0.0 copy-start.7
  112.7 1.8 fusion.16
  114.6 3.4 %convolution_convert_fusion = bf16[8,64,2880]{2,1,0:T(8,128)(2,1)} fusion(bf16[8,64,384]{2,1,0:T(8,128)(2,1)S(1)} %bitcast.59, bf16[1,384,2880]{1,2,0:T(8,128)(2,1)S(1)} %copy-done.7), kind=kOutput, calls=%fused_computation.2 | convolution fusion | flops 1133936640 | bytes 5554176 | tf_op jit(solution)/shard_map/dot_general | solution.py:63
  118.0 0.0 reduce-scatter.5.cloned.1.call-update
  118.0 37.2 %reduce-scatter.5.cloned.1.call-done = bf16[8,16,2880]{2,1,0:T(8,128)(2,1)} async-done(((bf16[8,64,2880]{2,1,0:T(8,128)(2,1)}), bf16[8,16,2880]{2,1,0:T(8,128)(2,1)}) %reduce-scatter.5.cloned.1.call-update) | async-done | bytes 737296 | tf_op jit(solution)/shard_map/reduce_scatter | solution.py:131
  155.2 5.5 %all-to-all-start.1 = ((bf16[8,16,2880]{2,1,0:T(8,128)(2,1)}), bf16[8,16,2880]{2,1,0:T(8,128)(2,1)}, u32[]{:S(2)}, u32[]{:S(2)}) async-start(bf16[8,16,2880]{2,1,0:T(8,128)(2,1)} %reduce-scatter.5.cloned.1.call-done), calls=%async_computation.3 | async-start | bytes 1507328 | tf_op jit(solution)/shard_map/all_to_all | solution.py:134
  160.7 0.1 fusion.38
  160.9 0.1 copy.22
  161.0 19.1 %all-to-all-done.1 = bf16[8,16,2880]{2,1,0:T(8,128)(2,1)} async-done(((bf16[8,16,2880]{2,1,0:T(8,128)(2,1)}), bf16[8,16,2880]{2,1,0:T(8,128)(2,1)}, u32[]{:S(2)}, u32[]{:S(2)}) %all-to-all-start.1) | async-done | bytes 737312 | tf_op jit(solution)/shard_map/all_to_all | solution.py:134
  180.1 2.4 %convert_element_type.66 = f32[8,16,2880]{2,1,0:T(8,128)} convert(bf16[8,16,2880]{2,1,0:T(8,128)(2,1)} %all-to-all-done.1) | non-fusion elementwise | flops 368640 | bytes 2211840 | tf_op jit(solution)/shard_map/convert_element_type | solution.py:136
  182.5 3.1 %gather_fusion = f32[64,2880]{1,0:T(8,128)} fusion(f32[8,16,2880]{2,1,0:T(8,128)} %convert_element_type.66, s32[64]{0:T(128)S(1)} %bitcast.56), kind=kCustom, calls=%fused_computation | custom fusion | bytes 1475072 | tf_op jit(solution)/shard_map/gather | solution.py:137
  185.5 2.2 %reshape.306 = f32[16,4,2880]{2,1,0:T(4,128)} reshape(f32[64,2880]{1,0:T(8,128)} %gather_fusion) | data formatting | bytes 1474560 | tf_op jit(solution)/shard_map/reshape | solution.py:137
  187.8 1.7 multiply_reduce_fusion
  189.4 1.6 add_convert_fusion
  (24 shorter events, 0.2 us)
Async XLA Ops:
  6.5 6.5 %copy-start = (bf16[512,2880]{0,1:T(8,128)(2,1)S(1)}, bf16[512,2880]{0,1:T(8,128)(2,1)}, u32[]{:S(2)}) copy-start(bf16[512,2880]{0,1:T(8,128)(2,1)} %param.20) | copy-start | bytes 8847364
  6.5 31.9 %reduce-scatter.3.cloned.1.call-start = ((), (), s32[]{:S(2)}) async-start(), calls=%async_computation.4 | async-start | bytes 471040 | tf_op jit(solution)/shard_map/reduce_scatter | solution.py:92
  9.3 2.5 %copy-start.8 = (bf16[8,1,64,1024]{3,2,1,0:T(8,128)(2,1)S(1)}, bf16[8,1,64,1024]{3,2,1,0:T(8,128)(2,1)}, u32[]{:S(2)}) copy-start(bf16[8,1,64,1024]{3,2,1,0:T(8,128)(2,1)} %param.18) | copy-start | bytes 3145732
  11.9 0.8 copy-start.3
  12.9 2.0 %copy-start.4 = (s32[64,4]{0,1:T(4,128)S(1)}, s32[64,4]{0,1:T(4,128)}, u32[]{:S(2)}) copy-start(s32[64,4]{0,1:T(4,128)} %param.22) | copy-start | bytes 3076
  14.8 93.5 %all-gather.2.cloned.1.call-start = ((), (), s32[]{:S(2)}) async-start(), calls=%async_computation.5 | async-start | bytes 3768320 | tf_op jit(solution)/shard_map/all_gather | solution.py:121
  82.2 73.0 %reduce-scatter.5.cloned.1.call-start = ((), (), s32[]{:S(2)}) async-start(), calls=%async_computation.6 | async-start | bytes 3768320 | tf_op jit(solution)/shard_map/reduce_scatter | solution.py:131
  108.3 4.4 %copy-start.5 = (bf16[8,64,2880]{2,1,0:T(8,128)(2,1)S(1)}, bf16[8,64,2880]{2,1,0:T(8,128)(2,1)}, u32[]{:S(2)}) copy-start(bf16[8,64,2880]{2,1,0:T(8,128)(2,1)} %all-gather.2.cloned.1.call-done) | copy-start | bytes 8847364
  108.3 4.4 %copy-start.6 = (bf16[1,2880,384]{2,1,0:T(8,128)(2,1)S(1)}, bf16[1,2880,384]{2,1,0:T(8,128)(2,1)}, u32[]{:S(2)}) copy-start(bf16[1,2880,384]{2,1,0:T(8,128)(2,1)} %param.24) | copy-start | bytes 6635524
  112.7 1.8 copy-start.7
  118.0 42.7 %copy-start.2 = (bf16[2880,8]{0,1:T(8,128)(2,1)S(1)}, bf16[2880,8]{0,1:T(8,128)(2,1)}, u32[]{:S(2)}) copy-start(bf16[2880,8]{0,1:T(8,128)(2,1)} %param.21) | copy-start | bytes 138244
  155.2 24.9 %all-to-all-start.1 = ((bf16[8,16,2880]{2,1,0:T(8,128)(2,1)}), bf16[8,16,2880]{2,1,0:T(8,128)(2,1)}, u32[]{:S(2)}, u32[]{:S(2)}) async-start(bf16[8,16,2880]{2,1,0:T(8,128)(2,1)} %reduce-scatter.5.cloned.1.call-done), calls=%async_computation.3 | async-start | bytes 1507328 | tf_op jit(solution)/shard_map/all_to_all | solution.py:134
  185.5 3.9 %copy-start.1 = (bf16[16,2880]{1,0:T(8,128)(2,1)S(1)}, bf16[16,2880]{1,0:T(8,128)(2,1)}, u32[]{:S(2)}) copy-start(bf16[16,2880]{1,0:T(8,128)(2,1)} %reduce-scatter.3.cloned.1.call-done) | copy-start | bytes 276484
Sparse Core Ops, SparseCore 0:
  14.9 23.4 reduce-scatter.2
  82.3 25.9 all-gather.1
  118.1 37.0 reduce-scatter.4
where the time goes:
time: 199 us; the launch traced here: 198 us
  waiting for transfers between devices  105 us (53%)
  blocking collectives  24.7 us (12%)
  local copies, waits for them, and re-layouts  23.7 us (12%)
  matrix products  15.2 us (8%)
  between operations  13.3 us (7%)
  other arithmetic  9.68 us (5%)
  starting transfers between devices  5.59 us (3%)
    reduce_scatter x1, waiting for transfers between devices, body(): lax.psum_scatter(grouped.astype(jnp.bfloat16), 'tp', scatter_dimension=1,...  37.2 us
    all_gather x1, waiting for transfers between devices, body(): lax.all_gather(lax.all_to_all(outgoing, 'ep', split_axis=0, concat_axis=0...  26.1 us
    all_to_all x1, blocking collectives, body(): lax.all_to_all(outgoing, 'ep', split_axis=0, concat_axis=0, tiled=True)  24.7 us
    reduce_scatter x1, waiting for transfers between devices, body(): lax.psum_scatter(partial_value.astype(jnp.bfloat16), 'tp', scatter_dimens...  22.9 us
    all_to_all x1, waiting for transfers between devices, body(): lax.all_to_all(group_total.astype(jnp.bfloat16), 'ep', split_axis=0, conc...  19.1 us
    scatter x1, local copies, waits for them, and re-layouts, body(): outgoing.at[flat_routes, slot_index]  13.9 us
    all_to_all x1, starting transfers between devices, body(): lax.all_to_all(group_total.astype(jnp.bfloat16), 'ep', split_axis=0, conc...  5.5 us
    dot_general x1, matrix products, expert_apply(): jnp.dot(flat_rows, w_gate[0], preferred_element_type=jnp.float32)  4.41 us
  transfers between devices with their start and end apart: 4, of which 4 were waited for; matrix products, arithmetic and copies ran while one was open for 0% of the time, Pallas kernels for 0%

commit v1 on v0

--- a/solution.py
+++ b/solution.py
@@ -64,6 +64,28 @@
     return partial_out.reshape(received.shape[0], received.shape[1], width)
 
 
+def dense_mix(residual, normed, weights, matches, w_gate, w_up, w_down):
+    width = normed.shape[1]
+    experts = matches.shape[2]
+    dense = jnp.sum(jnp.where(matches, weights[:, :, None], 0.0), 1)
+    high = dense.astype(jnp.bfloat16)
+    low = (dense - high.astype(jnp.float32)).astype(jnp.bfloat16)
+    rows = lax.all_gather(
+        jnp.concatenate([normed, high, low], 1), ("ep", "tp"), axis=0, tiled=True
+    )
+    tokens = rows[:, :width]
+    shares = rows[:, width : width + experts].astype(jnp.float32) + rows[
+        :, width + experts :
+    ].astype(jnp.float32)
+    mine = jnp.arange(experts) == lax.axis_index("ep")
+    share = jnp.sum(jnp.where(mine[None, :], shares, 0.0), 1, keepdims=True)
+    partial_out = expert_apply(tokens[None], w_gate, w_up, w_down)[0]
+    mixture = lax.psum_scatter(
+        (share * partial_out).astype(jnp.bfloat16), ("ep", "tp"), scatter_dimension=0, tiled=True
+    )
+    return (residual + mixture.astype(jnp.float32)).astype(jnp.bfloat16)
+
+
 def body(
     hidden,
     queries,
@@ -106,6 +128,8 @@
     picked = jnp.sum(jnp.where(matches, logits[:, None, :], 0.0), -1)
     picked_exp = jnp.exp(picked)
     weights = picked_exp / jnp.sum(picked_exp, -1, keepdims=True)
+    if capacity >= block_rows:
+        return dense_mix(residual, normed, weights, matches, w_gate, w_up, w_down)
     flat_routes = local_routes.reshape(-1)
     one_hot = (
         flat_routes.reshape(block_count, block_rows * top_count)[:, :, None]

time: 199 us -> 264 us (1.33)
  waiting for transfers between devices: 105 us -> 221 us
  blocking collectives: 24.7 us -> 0 us
  local copies, waits for them, and re-layouts: 23.7 us -> 2.14 us
  starting transfers between devices: 5.59 us -> 0.09 us
  matrix products: 15.2 us -> 20.1 us
  other arithmetic: 9.68 us -> 6.42 us
    reduce_scatter x1, waiting for transfers between devices: 37.2 us -> 139 us  [dense_mix(): lax.psum_scatter((share * partial_out).astype(jnp.bfloat16), ('ep', 'tp')...]
    all_gather x1, waiting for transfers between devices: 26.1 us -> 58.9 us  [dense_mix(): lax.all_gather(jnp.concatenate([normed, high, low], 1), ('ep', 'tp'), axi...]
    all_to_all x1 -> x0, blocking collectives: 24.7 us -> none  [body(): lax.all_to_all(outgoing, 'ep', split_axis=0, concat_axis=0, tiled=True)]
    all_to_all x1 -> x0, waiting for transfers between devices: 19.1 us -> none  [body(): lax.all_to_all(group_total.astype(jnp.bfloat16), 'ep', split_axis=0, conc...]
    scatter x1 -> x0, local copies, waits for them, and re-layouts: 13.9 us -> none  [body(): outgoing.at[flat_routes, slot_index]]
    all_to_all x1 -> x0, starting transfers between devices: 5.5 us -> none  [body(): lax.all_to_all(group_total.astype(jnp.bfloat16), 'ep', split_axis=0, conc...]
    dot_general x1, matrix products: 3.39 us -> 8.52 us  [expert_apply(): jnp.dot(activated, w_down[0], preferred_element_type=jnp.float32)]
    reshape x3 -> x0, local copies, waits for them, and re-layouts: 3.48 us -> none  [the longest x1 2.24 us: body(): routed = returned[flat_routes, slot_index].reshape(-1, top_count, width)]
  transfers between devices with their start and end apart: 4 -> 3, of which waited for: 4 -> 3; matrix products, arithmetic and copies ran while one was open for 0% -> 0% of each run, Pallas kernels for 0% -> 0%
where the time goes in v1:
time: 264 us; the launch traced here: 263 us
  waiting for transfers between devices  221 us (84%)
  matrix products  20.1 us (8%)
  between operations  13.3 us (5%)
  other arithmetic  6.42 us (2%)
    reduce_scatter x1, waiting for transfers between devices, dense_mix(): lax.psum_scatter((share * partial_out).astype(jnp.bfloat16), ('ep', 'tp')...  139 us
    all_gather x1, waiting for transfers between devices, dense_mix(): lax.all_gather(jnp.concatenate([normed, high, low], 1), ('ep', 'tp'), axi...  58.9 us
    reduce_scatter x1, waiting for transfers between devices, body(): lax.psum_scatter(partial_value.astype(jnp.bfloat16), 'tp', scatter_dimens...  23.5 us
    dot_general x1, matrix products, expert_apply(): jnp.dot(activated, w_down[0], preferred_element_type=jnp.float32)  8.52 us
  transfers between devices with their start and end apart: 3, of which 3 were waited for; matrix products, arithmetic and copies ran while one was open for 0% of the time, Pallas kernels for 0%

profile of v1, /device:TPU:0, one launch (start us, length us, event | category | flops | bytes accessed | tf_op | source)
XLA Modules:
  0.0 263.4 jit_solution(407085920326218181)
XLA Ops:
  6.5 0.0 copy-start
  6.5 0.0 reduce-scatter.3.cloned.1.call-start
  6.6 0.9 iota_compare_fusion
  7.4 1.0 reshape.162
  8.4 0.9 fusion.51
  9.3 0.0 copy-start.5
  9.3 1.9 fusion.7
  11.2 0.6 fusion.8
  11.9 0.0 copy-done.5
  11.9 0.0 copy-start.3
  11.9 0.7 fusion.31
  12.6 0.0 copy-done.3
  12.6 0.0 copy-start.4
  12.7 0.0 copy-start.2
  12.7 0.2 fusion.29
  12.9 0.1 convert_element_type.57
  13.1 0.0 copy-done
  13.1 1.7 convolution_convert_fusion
  14.8 0.0 reduce-scatter.3.cloned.1.call-update
  14.8 0.0 all-gather.2.cloned.1.call-start
  14.9 0.0 copy-done.4
  14.9 0.1 constant_dynamic-slice_fusion
  15.0 23.5 %reduce-scatter.3.cloned.1.call-done = bf16[16,2880]{1,0:T(8,128)(2,1)} async-done(((bf16[64,2880]{1,0:T(8,128)(2,1)}), bf16[16,2880]{1,0:T(8,128)(2,1)}) %reduce-scatter.3.cloned.1.call-update) | async-done | bytes 92176 | tf_op jit(solution)/shard_map/reduce_scatter | solution.py:114
  38.5 0.0 copy-done.2
  38.5 1.0 multiply_reduce_fusion
  39.5 1.0 multiply_convert_fusion.1
  40.5 0.9 fusion.52
  41.5 0.1 copy.19
  41.6 0.1 copy.18
  41.7 0.7 concatenate.3
  42.4 0.0 all-gather.2.cloned.1.call-update
  42.5 0.0 reduce-scatter.5.cloned.1.call-start
  42.5 58.9 %all-gather.2.cloned.1.call-done = bf16[512,2896]{1,0:T(8,128)(2,1)} async-done(((bf16[16,2896]{1,0:T(8,128)(2,1)}), bf16[512,2896]{1,0:T(8,128)(2,1)}) %all-gather.2.cloned.1.call-update) | async-done | bytes 2965520 | tf_op jit(solution)/shard_map/all_gather | solution.py:73
  101.5 1.2 select_reduce_fusion
  102.7 5.2 %fusion = f32[512,384]{1,0:T(8,128)} fusion(bf16[512,2896]{1,0:T(8,128)(2,1)} %all-gather.2.cloned.1.call-done, bf16[1,2880,384]{2,1,0:T(8,128)(2,1)} %param.23), kind=kOutput, calls=%fused_computation.2 | convolution fusion | flops 1132462080 | bytes 5963776 | tf_op jit(solution)/shard_map/dot_general | solution.py:58
  107.9 8.5 %multiply_convert_fusion = bf16[512,2880]{1,0:T(8,128)(2,1)} fusion(f32[512]{0:T(512)S(1)} %select_reduce_fusion, bf16[1,384,2880]{1,2,0:T(8,128)(2,1)} %param.25, f32[512,384]{1,0:T(8,128)} %fusion, bf16[1,2880,384]{2,1,0:T(8,128)(2,1)} %param.24, bf16[512,2896]{1,0:T(8,128)(2,1)} %all-gather.2.cloned.1.call-done), kind=kOutput, calls=%fused_computation | convolution fusion | flops 2269446144 | bytes 11126784 | tf_op jit(solution)/shard_map/dot_general | solution.py:63
  116.4 0.0 copy-start.1
  116.4 0.0 reduce-scatter.5.cloned.1.call-update
  116.4 138.9 %reduce-scatter.5.cloned.1.call-done = bf16[16,2880]{1,0:T(8,128)(2,1)} async-done(((bf16[512,2880]{1,0:T(8,128)(2,1)}), bf16[16,2880]{1,0:T(8,128)(2,1)}) %reduce-scatter.5.cloned.1.call-update) | async-done | bytes 92176 | tf_op jit(solution)/shard_map/reduce_scatter | solution.py:83
  255.3 0.0 copy-done.1
  255.3 1.6 add_convert_fusion
  (12 shorter events, 0.1 us)
Async XLA Ops:
  6.5 6.5 %copy-start = (bf16[512,2880]{0,1:T(8,128)(2,1)S(1)}, bf16[512,2880]{0,1:T(8,128)(2,1)}, u32[]{:S(2)}) copy-start(bf16[512,2880]{0,1:T(8,128)(2,1)} %param.20) | copy-start | bytes 8847364
  6.5 31.9 %reduce-scatter.3.cloned.1.call-start = ((), (), s32[]{:S(2)}) async-start(), calls=%async_computation.2 | async-start | bytes 471040 | tf_op jit(solution)/shard_map/reduce_scatter | solution.py:114
  9.3 2.5 copy-start.5
  11.9 0.8 copy-start.3
  12.6 2.3 copy-start.4
  12.7 25.8 %copy-start.2 = (bf16[64,2880]{1,0:T(8,128)(2,1)S(1)}, bf16[64,2880]{1,0:T(8,128)(2,1)}, u32[]{:S(2)}) copy-start(bf16[64,2880]{1,0:T(8,128)(2,1)} %param.13) | copy-start | bytes 1105924
  14.8 86.6 %all-gather.2.cloned.1.call-start = ((), (), s32[]{:S(2)}) async-start(), calls=%async_computation.3 | async-start | bytes 3108864 | tf_op jit(solution)/shard_map/all_gather | solution.py:73
  42.5 212.9 %reduce-scatter.5.cloned.1.call-start = ((), (), s32[]{:S(2)}) async-start(), calls=%async_computation.4 | async-start | bytes 3108864 | tf_op jit(solution)/shard_map/reduce_scatter | solution.py:83
  116.4 139.0 %copy-start.1 = (bf16[16,2880]{1,0:T(8,128)(2,1)S(1)}, bf16[16,2880]{1,0:T(8,128)(2,1)}, u32[]{:S(2)}) copy-start(bf16[16,2880]{1,0:T(8,128)(2,1)} %reduce-scatter.3.cloned.1.call-done) | copy-start | bytes 276484
Sparse Core Ops, SparseCore 0:
  15.0 23.4 reduce-scatter.2
  42.6 58.8 all-gather.1
  116.5 138.7 reduce-scatter.4

commit v2 on v0

--- a/solution.py
+++ b/solution.py
@@ -1,7 +1,14 @@
+import functools
+
 import jax
 import jax.numpy as jnp
 from jax import lax
+from jax.experimental import pallas as pl
+from jax.experimental.pallas import tpu as pltpu
 from jax.sharding import PartitionSpec as P
+
+LANES = 128
+MESH = pl.DeviceIdType.MESH
 
 
 def attend(queries, new_keys, new_values, key_cache, value_cache, cache_lengths):
@@ -62,6 +69,286 @@
     )
     partial_out = jnp.dot(activated, w_down[0], preferred_element_type=jnp.float32)
     return partial_out.reshape(received.shape[0], received.shape[1], width)
+
+
+def layer_kernel(
+    ep_size,
+    experts,
+    part_ref,
+    hidden_ref,
+    router_ref,
+    mask_ref,
+    gate_hbm,
+    up_hbm,
+    down_hbm,
+    out_ref,
+    got,
+    res,
+    rows,
+    mixed,
+    core_in,
+    b_in,
+    a_in,
+    z_in,
+    w_gate,
+    w_up,
+    w_down,
+    load_sem,
+    first_send,
+    first_recv,
+    gather_send,
+    gather_recv,
+    core_send,
+    core_recv,
+    sum_send,
+    sum_recv,
+):
+    tp_size, block_rows, width = part_ref.shape
+    padded = rows.shape[2]
+    base = width // LANES * LANES
+    offset = width - base
+    line = ep_size // 2
+    lane_slots = 4 * line
+    ep = lax.axis_index("ep")
+    tp = lax.axis_index("tp")
+    x = ep % 2
+    z = ep // 2
+    core = tp % 2
+    y = tp // 2
+    x_step = 1 - 2 * x
+    y_step = 2 - 4 * y
+    partner = (ep, tp + 1 - 2 * core)
+    a_dev = (ep + (1 - core) * x_step, tp + core * y_step)
+    b_dev = (ep + core * x_step, tp + (1 - core) * y_step)
+
+    def z_dev(k):
+        return (((z + k) % line) * 2 + x, tp)
+
+    loads = [
+        pltpu.make_async_copy(gate_hbm.at[0], w_gate.at[pl.ds(0, width)], load_sem.at[0]),
+        pltpu.make_async_copy(up_hbm.at[0], w_up.at[pl.ds(0, width)], load_sem.at[1]),
+        pltpu.make_async_copy(down_hbm.at[0], w_down, load_sem.at[2]),
+    ]
+    for load in loads:
+        load.start()
+
+    peers = [(ep, (tp + k) % tp_size) for k in range(1, tp_size)]
+    peers += [(ep + x_step, tp)] + [z_dev(k) for k in range(1, line)]
+    barrier = pltpu.get_barrier_semaphore()
+    for peer in peers:
+        pl.semaphore_signal(barrier, inc=1, device_id=peer, device_id_type=MESH)
+    pl.semaphore_wait(barrier, len(peers))
+
+    def send(src, dst, send_sem, recv_sem, index, device):
+        copy = pltpu.make_async_remote_copy(
+            src_ref=src,
+            dst_ref=dst,
+            send_sem=send_sem.at[index],
+            recv_sem=recv_sem.at[index],
+            device_id=device,
+            device_id_type=MESH,
+        )
+        copy.start()
+        return copy
+
+    firsts = []
+    for k in (2, 1, 3):
+        target = (tp + k) % tp_size
+        firsts.append(
+            send(part_ref.at[target], got.at[k - 1], first_send, first_recv, k - 1, (ep, target))
+        )
+    w_gate[width:, :] = jnp.zeros((padded - width, w_gate.shape[1]), w_gate.dtype)
+    w_up[width:, :] = jnp.zeros((padded - width, w_up.shape[1]), w_up.dtype)
+    res[:, base:] = jnp.zeros((block_rows, padded - base), jnp.float32)
+    own = part_ref[tp].astype(jnp.float32)
+    for copy in firsts:
+        copy.wait_recv()
+    for k in range(tp_size - 1):
+        own = own + got[k].astype(jnp.float32)
+    own = own.astype(jnp.bfloat16).astype(jnp.float32) + hidden_ref[...].astype(jnp.float32)
+    res[:, :width] = own
+    scale = lax.rsqrt(jnp.sum(own * own, -1, keepdims=True) * (1.0 / width) + 1e-05)
+    normed = (res[...] * scale).astype(jnp.bfloat16)
+    logits = jnp.dot(normed, router_ref[...], preferred_element_type=jnp.float32)
+    lane = lax.broadcasted_iota(jnp.int32, (block_rows, LANES), 1)
+    picked_exp = jnp.where(mask_ref[...] > 0, jnp.exp(logits), 0.0)
+    second = lane >= offset + experts
+    denom = jnp.sum(jnp.where(second, 0.0, picked_exp), -1, keepdims=True)
+    weights = picked_exp / denom
+    high = weights.astype(jnp.bfloat16).astype(jnp.float32)
+    tail = jnp.where(second, weights - high, high)
+    tail = jnp.where(lane < offset, normed[:, base:].astype(jnp.float32), tail)
+    rows[0, :, :base] = normed[:, :base]
+    rows[0, :, base:] = tail.astype(jnp.bfloat16)
+
+    moves = {}
+
+    def spread(slot, device, source):
+        moves[slot] = send(
+            rows.at[source], rows.at[slot], gather_send, gather_recv, slot, device
+        )
+
+    def forward(slot):
+        if slot < line:
+            spread(line + slot, a_dev, slot)
+        if slot < 2 * line:
+            spread(2 * line + slot, b_dev, slot)
+        spread(lane_slots + slot, partner, slot)
+
+    near = [k for k in range(1, line) if k in (1, line - 1)]
+    far = [k for k in range(1, line) if k not in near]
+    order = near + far
+    for k in order:
+        spread(line - k, z_dev(k), 0)
+    forward(0)
+    for slot in [line - k for k in order] + list(range(line, 2 * line)):
+        moves[slot].wait_recv()
+        forward(slot)
+    for load in loads:
+        load.wait()
+    share_lane = lax.broadcasted_iota(jnp.int32, (2 * line * block_rows, LANES), 1)
+    chosen = (share_lane == offset + ep) | (share_lane == offset + experts + ep)
+
+    def expert(start):
+        count = 2 * line
+        held = rows[start : start + count].reshape(count * block_rows, padded)
+        gate = jnp.dot(held, w_gate[...], preferred_element_type=jnp.float32)
+        up = jnp.dot(held, w_up[...], preferred_element_type=jnp.float32)
+        active = ((up + 1.0) * gate * jax.nn.sigmoid(1.702 * gate)).astype(jnp.bfloat16)
+        share = jnp.sum(
+            jnp.where(chosen, held[:, base:].astype(jnp.float32), 0.0), -1, keepdims=True
+        )
+        step = 6 * LANES
+        for low in range(0, width, step):
+            size = min(step, width - low)
+            out = jnp.dot(
+                active, w_down[:, low : low + size], preferred_element_type=jnp.float32
+            )
+            mixed[start : start + count, :, low : low + size] = (
+                (share * out).astype(jnp.bfloat16).reshape(count, block_rows, size)
+            )
+
+    half = 2 * line
+    expert(0)
+    for slot in range(half):
+        moves[lane_slots + slot].wait_recv()
+    expert(lane_slots)
+    for slot in range(half, 2 * half):
+        moves[slot].wait_recv()
+        forward(slot)
+    expert(half)
+    for slot in range(half, 2 * half):
+        moves[lane_slots + slot].wait_recv()
+    expert(lane_slots + half)
+
+    crossing = {}
+    for quarter in (3, 2, 1, 0):
+        crossing[quarter] = send(
+            mixed.at[pl.ds(lane_slots + quarter * line, line)],
+            core_in.at[pl.ds(quarter * line, line)],
+            core_send,
+            core_recv,
+            quarter,
+            partner,
+        )
+
+    sums = {}
+
+    def reduce_send(slot, parts, dst, device):
+        total = mixed[slot].astype(jnp.float32) + core_in[slot].astype(jnp.float32)
+        for part in parts:
+            total = total + part.astype(jnp.float32)
+        mixed[slot] = total.astype(jnp.bfloat16)
+        sums[slot] = send(mixed.at[slot], dst, sum_send, sum_recv, slot, device)
+
+    for quarter in (3, 2):
+        crossing[quarter].wait_recv()
+        for slot in range(quarter * line, (quarter + 1) * line):
+            reduce_send(slot, [], b_in.at[slot - half], b_dev)
+    crossing[1].wait_recv()
+    for slot in range(line, half):
+        sums[half + slot].wait_recv()
+        reduce_send(slot, [b_in[slot]], a_in.at[slot - line], a_dev)
+    crossing[0].wait_recv()
+    for slot in far + near:
+        sums[half + slot].wait_recv()
+        sums[line + slot].wait_recv()
+        reduce_send(slot, [b_in[slot], a_in[slot]], z_in.at[slot - 1], z_dev(slot))
+    sums[half].wait_recv()
+    sums[line].wait_recv()
+    total = res[:, :width] + mixed[0].astype(jnp.float32) + core_in[0].astype(jnp.float32)
+    total = total + b_in[0].astype(jnp.float32) + a_in[0].astype(jnp.float32)
+    for slot in far + near:
+        sums[slot].wait_recv()
+        total = total + z_in[slot - 1].astype(jnp.float32)
+    out_ref[...] = total.astype(jnp.bfloat16)
+    for copy in (
+        firsts + list(moves.values()) + list(crossing.values()) + list(sums.values())
+    ):
+        copy.wait_send()
+
+
+def fused_layer(partial_value, hidden, w_router, routes, w_gate, w_up, w_down):
+    ep_size = lax.axis_size("ep")
+    tp_size = lax.axis_size("tp")
+    block_rows, width = hidden.shape
+    experts = w_router.shape[1]
+    hidden_share = w_gate.shape[2]
+    base = width // LANES * LANES
+    offset = width - base
+    padded = base + LANES
+    line = ep_size // 2
+    slots = 8 * line
+    room = LANES - offset - 2 * experts
+    router = jnp.pad(
+        jnp.concatenate([w_router, w_router], 1), ((0, padded - width), (offset, room))
+    )
+    named = jnp.any(routes[:, :, None] == jnp.arange(experts)[None, None, :], 1)
+    named = named.astype(jnp.float32)
+    mask = jnp.pad(jnp.concatenate([named, named], 1), ((0, 0), (offset, room)))
+    vmem = pl.BlockSpec(memory_space=pltpu.VMEM)
+    any_space = pl.BlockSpec(memory_space=pl.ANY)
+    dma = pltpu.SemaphoreType.DMA
+    bf16 = jnp.bfloat16
+    return pl.pallas_call(
+        functools.partial(layer_kernel, ep_size, experts),
+        out_shape=jax.ShapeDtypeStruct((block_rows, width), bf16),
+        in_specs=[vmem] * 4 + [any_space] * 3,
+        out_specs=vmem,
+        scratch_shapes=[
+            pltpu.VMEM((tp_size - 1, block_rows, width), bf16),
+            pltpu.VMEM((block_rows, padded), jnp.float32),
+            pltpu.VMEM((slots, block_rows, padded), bf16),
+            pltpu.VMEM((slots, block_rows, width), bf16),
+            pltpu.VMEM((slots // 2, block_rows, width), bf16),
+            pltpu.VMEM((slots // 4, block_rows, width), bf16),
+            pltpu.VMEM((slots // 8, block_rows, width), bf16),
+            pltpu.VMEM((line - 1, block_rows, width), bf16),
+            pltpu.VMEM((padded, hidden_share), bf16),
+            pltpu.VMEM((padded, hidden_share), bf16),
+            pltpu.VMEM((hidden_share, width), bf16),
+            dma((3,)),
+            dma((tp_size - 1,)),
+            dma((tp_size - 1,)),
+            dma((slots,)),
+            dma((slots,)),
+            dma((4,)),
+            dma((4,)),
+            dma((slots // 2,)),
+            dma((slots // 2,)),
+        ],
+        compiler_params=pltpu.CompilerParams(
+            collective_id=0, has_side_effects=True, vmem_limit_bytes=48 * 1024 * 1024
+        ),
+    )(
+        partial_value.reshape(tp_size, block_rows, width),
+        hidden,
+        router,
+        mask,
+        w_gate,
+        w_up,
+        w_down,
+    )
 
 
 def body(
@@ -89,6 +376,17 @@
     start_row = tp_index * block_rows
     attended = attend(queries, new_keys, new_values, key_cache, value_cache, cache_lengths)
     partial_value = jnp.dot(attended, w_out, preferred_element_type=jnp.float32)
+    fits = width % LANES + 2 * experts <= LANES and experts == lax.axis_size("ep")
+    if capacity >= block_rows and tp_size == 4 and experts % 2 == 0 and experts > 2 and fits:
+        return fused_layer(
+            partial_value.astype(jnp.bfloat16),
+            lax.dynamic_slice_in_dim(hidden, start_row, block_rows, 0),
+            w_router,
+            lax.dynamic_slice_in_dim(routes, start_row, block_rows, 0),
+            w_gate,
+            w_up,
+            w_down,
+        )
     summed = lax.psum_scatter(
         partial_value.astype(jnp.bfloat16), "tp", scatter_dimension=0, tiled=True
     ).astype(jnp.float32)

time: 199 us -> 79.4 us (0.40)
  waiting for transfers between devices: 105 us -> 0 us
  Pallas kernels: 0 us -> 57.1 us
  blocking collectives: 24.7 us -> 0 us
  between operations: 13.3 us -> 0.12 us
  matrix products: 15.2 us -> 3.42 us
  local copies, waits for them, and re-layouts: 23.7 us -> 15.8 us
  other arithmetic: 9.68 us -> 2.44 us
  starting transfers between devices: 5.59 us -> 0 us
    reduce_scatter x2 -> x0, waiting for transfers between devices: 60 us -> none  [the longest x1 37.2 us: body(): lax.psum_scatter(grouped.astype(jnp.bfloat16), 'tp', scatter_dimension=1,...]
    pallas_call x0 -> x1, Pallas kernels: none -> 57.1 us  [fused_layer(): pl.pallas_call(functools.partial(layer_kernel, ep_size, experts), out_sha...]
    all_gather x1 -> x0, waiting for transfers between devices: 26.1 us -> none  [body(): lax.all_gather(lax.all_to_all(outgoing, 'ep', split_axis=0, concat_axis=0...]
    all_to_all x1 -> x0, blocking collectives: 24.7 us -> none  [body(): lax.all_to_all(outgoing, 'ep', split_axis=0, concat_axis=0, tiled=True)]
    all_to_all x1 -> x0, waiting for transfers between devices: 19.1 us -> none  [body(): lax.all_to_all(group_total.astype(jnp.bfloat16), 'ep', split_axis=0, conc...]
    scatter x1 -> x0, local copies, waits for them, and re-layouts: 13.9 us -> none  [body(): outgoing.at[flat_routes, slot_index]]
    dot_general x4 -> x0, matrix products: 9.75 us -> none  [the longest x1 4.41 us: expert_apply(): jnp.dot(flat_rows, w_gate[0], preferred_element_type=jnp.float32)]
    unnamed x18 -> x16, local copies, waits for them, and re-layouts: 0.04 us -> 9.22 us
  transfers between devices with their start and end apart: 4 -> 0, of which waited for: 4 -> 0; matrix products, arithmetic and copies ran while one was open for 0% -> 0% of each run, Pallas kernels for 0% -> 0%
where the time goes in v2:
time: 79.4 us; the launch traced here: 78.8 us
  Pallas kernels  57.1 us (72%)
  local copies, waits for them, and re-layouts  15.8 us (20%)
  matrix products  3.42 us (4%)
  other arithmetic  2.44 us (3%)
    pallas_call x1, Pallas kernels, fused_layer(): pl.pallas_call(functools.partial(layer_kernel, ep_size, experts), out_sha...  57.1 us
    unnamed x16, local copies, waits for them, and re-layouts  9.22 us
    pad x1, local copies, waits for them, and re-layouts, fused_layer(): jnp.pad(jnp.concatenate([w_router, w_router], 1), ((0, padded - width), (...  2.35 us

profile of v2, /device:TPU:0, one launch (start us, length us, event | category | flops | bytes accessed | tf_op | source)
XLA Modules:
  0.0 78.8 jit_solution(15218653826202721055)
XLA Ops:
  0.0 0.0 copy-start
  0.0 0.9 %constant_dynamic-slice_fusion = s32[16,4]{0,1:T(4,128)S(1)} fusion(s32[64,4]{0,1:T(4,128)} %param.22, s32[]{:T(128)S(6)} %select_n.26), kind=kLoop, calls=%fused_computation.33 | loop fusion | bytes 516 | tf_op jit(solution)/shard_map/dynamic_slice | solution.py:385
  0.9 0.1 copy.22
  1.0 0.1 pad_add_fusion
  1.1 0.1 pad_convert_fusion.mask_ref
  1.2 0.7 iota_compare_fusion
  1.9 0.9 %constant_dynamic-slice_fusion.1.hidden_ref = bf16[16,2880]{1,0:T(8,128)(2,1)S(1)} fusion(bf16[64,2880]{1,0:T(8,128)(2,1)} %param.13, s32[]{:T(128)S(6)} %select_n.26), kind=kLoop, calls=%fused_computation.34 | loop fusion | bytes 184324 | tf_op jit(solution)/shard_map/dynamic_slice | solution.py:383
  2.8 0.9 %pad_maximum_fusion = bf16[2880,16]{0,1:T(8,128)(2,1)S(1)} fusion(bf16[2880,8]{0,1:T(8,128)(2,1)} %param.21), kind=kLoop, calls=%fused_computation.15 | loop fusion | flops 184320 | bytes 138240 | tf_op jit(solution)/shard_map/concatenate | solution.py:304
  3.7 1.0 %reshape.132 = bf16[8,64,64]{2,1,0:T(8,128)(2,1)S(1)} reshape(bf16[64,512]{1,0:T(8,128)(2,1)} %param.14) | data formatting | bytes 131072 | tf_op jit(solution)/shard_map/reshape.2
  4.7 0.9 %fusion.17 = (f32[8,64]{1,0:T(8,128)S(1)}, f32[8,64,8]{1,2,0:T(8,128)S(1)}) fusion(bf16[8,64,64]{2,1,0:T(8,128)(2,1)S(1)} %reshape.132, bf16[64,64]{1,0:T(8,128)(2,1)} %param.15, pred[64,8]{0,1:T(8,128)(4,1)S(1)} %iota_compare_fusion.2), kind=kOutput, calls=%fused_computation.37 | convolution fusion | flops 536064 | bytes 92672 | tf_op jit(solution)/shard_map/skrd,sknd->skrn/dot_general | solution.py:35
  5.6 1.2 %copy.21 = bf16[2880,16]{1,0:T(8,128)(2,1)} copy(bf16[2880,16]{0,1:T(8,128)(2,1)S(1)} %pad_maximum_fusion) | data formatting | bytes 184320 | tf_op jit(solution)/shard_map/concatenate | solution.py:304
  6.8 0.0 copy-start.4
  6.8 2.4 %pad.10.router_ref = bf16[2944,128]{1,0:T(8,128)(2,1)} pad(bf16[2880,16]{1,0:T(8,128)(2,1)} %copy.21, bf16[]{:T(256)} %constant.40.clone.1), padding=0_64x64_48 | pad | bytes 845826 | tf_op jit(solution)/shard_map/jit(_pad)/pad | solution.py:303
  9.1 0.0 copy-done.4
  9.1 0.0 copy-start.6
  9.1 0.5 fusion
  9.7 0.6 fusion.1
  10.3 0.0 copy-done.6
  10.3 0.0 copy-start.5
  10.3 0.7 fusion.4
  11.1 0.0 copy-done.5
  11.1 0.2 fusion.2
  11.4 0.1 convert_element_type.25
  11.5 0.0 copy-done
  11.5 1.0 %convolution_convert_fusion = bf16[64,2880]{1,0:T(8,128)(2,1)S(1)} fusion(bf16[64,512]{1,0:T(8,128)(2,1)S(1)} %convert_element_type.25, bf16[512,2880]{0,1:T(8,128)(2,1)S(1)} %copy-done), kind=kOutput, calls=%fused_computation | convolution fusion | flops 188928000 | bytes 3383296 | tf_op jit(solution)/shard_map/dot_general | solution.py:378
  12.5 4.2 %copy.24.down_hbm = bf16[1,384,2880]{2,1,0:T(8,128)(2,1)} copy(bf16[1,384,2880]{1,2,0:T(8,128)(2,1)} %param.25) | data formatting | bytes 4423680 | tf_op args[12]
  16.7 0.0 copy-start.1
  16.7 1.1 %copy-done.1 = bf16[2944,128]{1,0:T(8,128)(2,1)S(1)} copy-done((bf16[2944,128]{1,0:T(8,128)(2,1)S(1)}, bf16[2944,128]{1,0:T(8,128)(2,1)}, u32[]{:S(2)}) %copy-start.1) | copy-done | bytes 753688
  17.8 0.0 copy-start.2
  17.8 1.6 %copy-done.2 = bf16[1,2880,384]{2,1,0:T(8,128)(2,1)S(1)} copy-done((bf16[1,2880,384]{2,1,0:T(8,128)(2,1)S(1)}, bf16[1,2880,384]{2,1,0:T(8,128)(2,1)}, u32[]{:S(2)}) %copy-start.2) | copy-done | bytes 2211864
  19.5 0.0 copy-start.3
  19.5 1.6 %copy-done.3 = bf16[1,2880,384]{2,1,0:T(8,128)(2,1)S(1)} copy-done((bf16[1,2880,384]{2,1,0:T(8,128)(2,1)S(1)}, bf16[1,2880,384]{2,1,0:T(8,128)(2,1)}, u32[]{:S(2)}) %copy-start.3) | copy-done | bytes 2211864
  21.1 57.1 %shard_map.127 = bf16[16,2880]{1,0:T(8,128)(2,1)S(1)} custom-call(bf16[4,16,2880]{2,1,0:T(8,128)(2,1)S(1)} %bitcast.21, bf16[16,2880]{1,0:T(8,128)(2,1)S(1)} %constant_dynamic-slice_fusion.1.hidden_ref, bf16[2944,128]{1,0:T(8,128)(2,1)S(1)} %copy-done.1, f32[16,128]{1,0:T(8,128)S(1)} %pad_convert_fusion.mask_ref, bf16[1,2880,384]{2,1,0:T(8,128)(2,1)S(1)} %copy-done.2, ...), custom_call_target="tpu_custom_call" | custom-call | tf_op jit(solution)/shard_map/pallas_call | solution.py:313
  78.2 0.6 copy.26
  (6 shorter events, 0.1 us)
Async XLA Ops:
  0.0 11.5 %copy-start = (bf16[512,2880]{0,1:T(8,128)(2,1)S(1)}, bf16[512,2880]{0,1:T(8,128)(2,1)}, u32[]{:S(2)}) copy-start(bf16[512,2880]{0,1:T(8,128)(2,1)} %param.20) | copy-start | bytes 8847364
  6.8 2.4 %copy-start.4 = (bf16[8,1,64,1024]{3,2,1,0:T(8,128)(2,1)S(1)}, bf16[8,1,64,1024]{3,2,1,0:T(8,128)(2,1)}, u32[]{:S(2)}) copy-start(bf16[8,1,64,1024]{3,2,1,0:T(8,128)(2,1)} %param.17) | copy-start | bytes 3145732
  9.1 1.2 %copy-start.6 = (bf16[8,1,64,1024]{3,2,1,0:T(8,128)(2,1)S(1)}, bf16[8,1,64,1024]{3,2,1,0:T(8,128)(2,1)}, u32[]{:S(2)}) copy-start(bf16[8,1,64,1024]{3,2,1,0:T(8,128)(2,1)} %param.18) | copy-start | bytes 3145732
  10.3 0.8 copy-start.5
  16.7 1.1 %copy-start.1 = (bf16[2944,128]{1,0:T(8,128)(2,1)S(1)}, bf16[2944,128]{1,0:T(8,128)(2,1)}, u32[]{:S(2)}) copy-start(bf16[2944,128]{1,0:T(8,128)(2,1)} %pad.10.router_ref) | copy-start | bytes 2260996
  17.8 1.6 %copy-start.2 = (bf16[1,2880,384]{2,1,0:T(8,128)(2,1)S(1)}, bf16[1,2880,384]{2,1,0:T(8,128)(2,1)}, u32[]{:S(2)}) copy-start(bf16[1,2880,384]{2,1,0:T(8,128)(2,1)} %gate_hbm.1) | copy-start | bytes 6635524
  19.5 1.6 %copy-start.3 = (bf16[1,2880,384]{2,1,0:T(8,128)(2,1)S(1)}, bf16[1,2880,384]{2,1,0:T(8,128)(2,1)}, u32[]{:S(2)}) copy-start(bf16[1,2880,384]{2,1,0:T(8,128)(2,1)} %up_hbm.1) | copy-start | bytes 6635524

commit v3 on v2

--- a/solution.py
+++ b/solution.py
@@ -77,7 +77,7 @@
     part_ref,
     hidden_ref,
     router_ref,
-    mask_ref,
+    routes_ref,
     gate_hbm,
     up_hbm,
     down_hbm,
@@ -93,6 +93,7 @@
     w_gate,
     w_up,
     w_down,
+    router,
     load_sem,
     first_send,
     first_recv,
@@ -159,20 +160,31 @@
         )
     w_gate[width:, :] = jnp.zeros((padded - width, w_gate.shape[1]), w_gate.dtype)
     w_up[width:, :] = jnp.zeros((padded - width, w_up.shape[1]), w_up.dtype)
+    router[...] = jnp.zeros(router.shape, router.dtype)
+    router[offset : offset + experts, :width] = router_ref[...]
+    router[offset + experts : offset + 2 * experts, :width] = router_ref[...]
     res[:, base:] = jnp.zeros((block_rows, padded - base), jnp.float32)
     own = part_ref[tp].astype(jnp.float32)
     for copy in firsts:
         copy.wait_recv()
     for k in range(tp_size - 1):
         own = own + got[k].astype(jnp.float32)
-    own = own.astype(jnp.bfloat16).astype(jnp.float32) + hidden_ref[...].astype(jnp.float32)
+    mine = pl.ds(pl.multiple_of(tp * block_rows, block_rows), block_rows)
+    own = own.astype(jnp.bfloat16).astype(jnp.float32) + hidden_ref[mine, :].astype(jnp.float32)
     res[:, :width] = own
     scale = lax.rsqrt(jnp.sum(own * own, -1, keepdims=True) * (1.0 / width) + 1e-05)
     normed = (res[...] * scale).astype(jnp.bfloat16)
-    logits = jnp.dot(normed, router_ref[...], preferred_element_type=jnp.float32)
+    logits = lax.dot_general(
+        normed, router[...], (((1,), (1,)), ((), ())), preferred_element_type=jnp.float32
+    )
     lane = lax.broadcasted_iota(jnp.int32, (block_rows, LANES), 1)
-    picked_exp = jnp.where(mask_ref[...] > 0, jnp.exp(logits), 0.0)
     second = lane >= offset + experts
+    lane_expert = jnp.where(second, lane - offset - experts, lane - offset)
+    routes = routes_ref[mine, :]
+    named = lane_expert == routes[:, 0:1]
+    for r in range(1, routes.shape[1]):
+        named = named | (lane_expert == routes[:, r : r + 1])
+    picked_exp = jnp.where(named, jnp.exp(logits), 0.0)
     denom = jnp.sum(jnp.where(second, 0.0, picked_exp), -1, keepdims=True)
     weights = picked_exp / denom
     high = weights.astype(jnp.bfloat16).astype(jnp.float32)
@@ -221,28 +233,21 @@
         step = 6 * LANES
         for low in range(0, width, step):
             size = min(step, width - low)
-            out = jnp.dot(
-                active, w_down[:, low : low + size], preferred_element_type=jnp.float32
+            out = lax.dot_general(
+                active,
+                w_down[low : low + size, :],
+                (((1,), (1,)), ((), ())),
+                preferred_element_type=jnp.float32,
             )
             mixed[start : start + count, :, low : low + size] = (
                 (share * out).astype(jnp.bfloat16).reshape(count, block_rows, size)
             )
 
     half = 2 * line
-    expert(0)
-    for slot in range(half):
-        moves[lane_slots + slot].wait_recv()
-    expert(lane_slots)
-    for slot in range(half, 2 * half):
-        moves[slot].wait_recv()
-        forward(slot)
-    expert(half)
-    for slot in range(half, 2 * half):
-        moves[lane_slots + slot].wait_recv()
-    expert(lane_slots + half)
-
     crossing = {}
-    for quarter in (3, 2, 1, 0):
+    sums = {}
+
+    def cross(quarter):
         crossing[quarter] = send(
             mixed.at[pl.ds(lane_slots + quarter * line, line)],
             core_in.at[pl.ds(quarter * line, line)],
@@ -252,8 +257,6 @@
             partner,
         )
 
-    sums = {}
-
     def reduce_send(slot, parts, dst, device):
         total = mixed[slot].astype(jnp.float32) + core_in[slot].astype(jnp.float32)
         for part in parts:
@@ -261,18 +264,35 @@
         mixed[slot] = total.astype(jnp.bfloat16)
         sums[slot] = send(mixed.at[slot], dst, sum_send, sum_recv, slot, device)
 
-    for quarter in (3, 2):
-        crossing[quarter].wait_recv()
-        for slot in range(quarter * line, (quarter + 1) * line):
-            reduce_send(slot, [], b_in.at[slot - half], b_dev)
+    expert(0)
+    for slot in range(half):
+        moves[lane_slots + slot].wait_recv()
+    expert(lane_slots)
+    cross(1)
+    cross(0)
+    for slot in range(half, 2 * half):
+        moves[slot].wait_recv()
+        forward(slot)
     crossing[1].wait_recv()
     for slot in range(line, half):
-        sums[half + slot].wait_recv()
-        reduce_send(slot, [b_in[slot]], a_in.at[slot - line], a_dev)
+        reduce_send(slot, [], a_in.at[slot - line], a_dev)
+    for slot in range(half, 2 * half):
+        moves[lane_slots + slot].wait_recv()
+    expert(lane_slots + half)
+    cross(3)
+    cross(2)
+    expert(half)
+    crossing[3].wait_recv()
+    for slot in range(3 * line, 4 * line):
+        reduce_send(slot, [], a_in.at[slot - half], a_dev)
+    crossing[2].wait_recv()
+    for slot in range(half, 3 * line):
+        sums[line + slot].wait_recv()
+        reduce_send(slot, [a_in[slot - line]], b_in.at[slot - half], b_dev)
     crossing[0].wait_recv()
     for slot in far + near:
+        sums[line + slot].wait_recv()
         sums[half + slot].wait_recv()
-        sums[line + slot].wait_recv()
         reduce_send(slot, [b_in[slot], a_in[slot]], z_in.at[slot - 1], z_dev(slot))
     sums[half].wait_recv()
     sums[line].wait_recv()
@@ -291,21 +311,14 @@
 def fused_layer(partial_value, hidden, w_router, routes, w_gate, w_up, w_down):
     ep_size = lax.axis_size("ep")
     tp_size = lax.axis_size("tp")
-    block_rows, width = hidden.shape
+    width = hidden.shape[1]
+    block_rows = hidden.shape[0] // tp_size
     experts = w_router.shape[1]
     hidden_share = w_gate.shape[2]
     base = width // LANES * LANES
-    offset = width - base
     padded = base + LANES
     line = ep_size // 2
     slots = 8 * line
-    room = LANES - offset - 2 * experts
-    router = jnp.pad(
-        jnp.concatenate([w_router, w_router], 1), ((0, padded - width), (offset, room))
-    )
-    named = jnp.any(routes[:, :, None] == jnp.arange(experts)[None, None, :], 1)
-    named = named.astype(jnp.float32)
-    mask = jnp.pad(jnp.concatenate([named, named], 1), ((0, 0), (offset, room)))
     vmem = pl.BlockSpec(memory_space=pltpu.VMEM)
     any_space = pl.BlockSpec(memory_space=pl.ANY)
     dma = pltpu.SemaphoreType.DMA
@@ -321,12 +334,13 @@
             pltpu.VMEM((slots, block_rows, padded), bf16),
             pltpu.VMEM((slots, block_rows, width), bf16),
             pltpu.VMEM((slots // 2, block_rows, width), bf16),
+            pltpu.VMEM((slots // 8, block_rows, width), bf16),
             pltpu.VMEM((slots // 4, block_rows, width), bf16),
-            pltpu.VMEM((slots // 8, block_rows, width), bf16),
             pltpu.VMEM((line - 1, block_rows, width), bf16),
             pltpu.VMEM((padded, hidden_share), bf16),
             pltpu.VMEM((padded, hidden_share), bf16),
-            pltpu.VMEM((hidden_share, width), bf16),
+            pltpu.VMEM((width, hidden_share), bf16),
+            pltpu.VMEM((LANES, padded), bf16),
             dma((3,)),
             dma((tp_size - 1,)),
             dma((tp_size - 1,)),
@@ -338,16 +352,16 @@
             dma((slots // 2,)),
         ],
         compiler_params=pltpu.CompilerParams(
-            collective_id=0, has_side_effects=True, vmem_limit_bytes=48 * 1024 * 1024
+            collective_id=0, has_side_effects=True, vmem_limit_bytes=67043328
         ),
     )(
         partial_value.reshape(tp_size, block_rows, width),
         hidden,
-        router,
-        mask,
+        w_router.T,
+        routes,
         w_gate,
         w_up,
-        w_down,
+        jnp.swapaxes(w_down, 1, 2),
     )
 
 
@@ -380,9 +394,9 @@
     if capacity >= block_rows and tp_size == 4 and experts % 2 == 0 and experts > 2 and fits:
         return fused_layer(
             partial_value.astype(jnp.bfloat16),
-            lax.dynamic_slice_in_dim(hidden, start_row, block_rows, 0),
+            hidden,
             w_router,
-            lax.dynamic_slice_in_dim(routes, start_row, block_rows, 0),
+            routes,
             w_gate,
             w_up,
             w_down,

time: 79.4 us -> 66.5 us (0.84)
  local copies, waits for them, and re-layouts: 15.8 us -> 4.05 us
  matrix products: 3.42 us -> 4.75 us
  Pallas kernels: 57.1 us -> 55.8 us
  other arithmetic: 2.44 us -> 1.41 us
    unnamed x16 -> x12, local copies, waits for them, and re-layouts: 9.22 us -> 2.93 us
    pad x1 -> x0, local copies, waits for them, and re-layouts: 2.35 us -> none  [fused_layer(): jnp.pad(jnp.concatenate([w_router, w_router], 1), ((0, padded - width), (...]
    dynamic_slice x2 -> x0, local copies, waits for them, and re-layouts: 1.8 us -> none  [the longest x1 0.91 us: body(): lax.dynamic_slice_in_dim(routes, start_row, block_rows, 0)]
    pallas_call x1, Pallas kernels: 57.1 us -> 55.8 us  [fused_layer(): pl.pallas_call(functools.partial(layer_kernel, ep_size, experts), out_sha...]
    dot_general x1, matrix products: 0.53 us -> 1.84 us  [attend(): jnp.einsum('skrd,skdl->skrl', query_block, key_cache, preferred_element_t...]
    concatenate x1 -> x0, local copies, waits for them, and re-layouts: 1.16 us -> none  [fused_layer(): jnp.concatenate([w_router, w_router], 1)]
    concatenate x2 -> x0, other arithmetic: 0.96 us -> none  [the longest x1 0.88 us: fused_layer(): jnp.concatenate([w_router, w_router], 1)]
where the time goes in v3:
time: 66.5 us; the launch traced here: 66.1 us
  Pallas kernels  55.8 us (84%)
  matrix products  4.75 us (7%)
  local copies, waits for them, and re-layouts  4.05 us (6%)
  other arithmetic  1.41 us (2%)
    pallas_call x1, Pallas kernels, fused_layer(): pl.pallas_call(functools.partial(layer_kernel, ep_size, experts), out_sha...  55.8 us
    unnamed x12, local copies, waits for them, and re-layouts  2.93 us
    dot_general x1, matrix products, attend(): jnp.einsum('skrd,skdl->skrl', query_block, key_cache, preferred_element_t...  1.84 us
    dot_general x1, matrix products, body(): partial_value = jnp.dot(attended, w_out, preferred_element_type=jnp.float32)  1.74 us

profile of v3, /device:TPU:0, one launch (start us, length us, event | category | flops | bytes accessed | tf_op | source)
XLA Modules:
  0.0 66.1 jit_solution(10801764956049345897)
XLA Ops:
  0.0 0.0 copy-start.2
  0.0 0.7 %iota_compare_fusion = pred[8,1024]{1,0:T(8,128)(4,1)S(1)} fusion(s32[8]{0:T(128)} %param.19), kind=kLoop, calls=%fused_computation.17 | loop fusion | flops 8192 | bytes 8224 | tf_op jit(solution)/shard_map/lt | solution.py:32
  0.7 1.0 %reshape.131 = bf16[8,64,64]{2,1,0:T(8,128)(2,1)S(1)} reshape(bf16[64,512]{1,0:T(8,128)(2,1)} %param.14) | data formatting | bytes 131072 | tf_op jit(solution)/shard_map/reshape.2
  1.7 0.0 copy-start.4
  1.7 1.8 %fusion = (f32[8,64]{1,0:T(8,128)S(1)}, f32[8,64,1024]{2,1,0:T(8,128)S(1)}) fusion(pred[8,1024]{1,0:T(8,128)(4,1)S(1)} %iota_compare_fusion, bf16[8,64,64]{2,1,0:T(8,128)(2,1)S(1)} %reshape.131, bf16[8,1,64,1024]{3,2,1,0:T(8,128)(2,1)} %param.17), kind=kOutput, calls=%fused_computation.4 | convolution fusion | flops 68681216 | bytes 3221504 | tf_op jit(solution)/shard_map/skrd,skdl->skrl/dot_general | solution.py:29
  3.6 0.0 copy-done.2
  3.6 0.2 fusion.16
  3.8 0.6 fusion.1
  4.5 0.0 copy-done.4
  4.5 0.0 copy-start.1
  4.5 0.0 copy-start
  4.5 0.7 %fusion.4 = f32[8,64,64]{2,1,0:T(8,128)S(1)} fusion(bf16[8,1,64,1024]{3,2,1,0:T(8,128)(2,1)S(1)} %copy-done.4, f32[8,64,1024]{2,1,0:T(8,128)S(1)} %get-tuple-element.6, f32[8,64]{1,0:T(8,128)S(1)} %add.17, f32[8,64]{1,0:T(8,128)S(1)} %max.8, pred[8,1024]{1,0:T(8,128)(4,1)S(1)} %iota_compare_fusion), kind=kOutput, calls=%fused_computation.10 | convolution fusion | flops 69730304 | bytes 3289088 | tf_op jit(solution)/shard_map/skrl,skdl->skrd/dot_general | solution.py:48
  5.3 0.0 copy-done.1
  5.3 0.0 copy-start.3
  5.3 0.2 fusion.2
  5.5 0.1 convert_element_type.20
  5.7 0.7 copy-done
  6.3 1.7 %convolution_convert_fusion = bf16[64,2880]{1,0:T(8,128)(2,1)} fusion(bf16[64,512]{1,0:T(8,128)(2,1)S(1)} %convert_element_type.20, bf16[512,2880]{0,1:T(8,128)(2,1)S(1)} %copy-done), kind=kOutput, calls=%fused_computation | convolution fusion | flops 188928000 | bytes 3383296 | tf_op jit(solution)/shard_map/dot_general | solution.py:392
  8.1 0.0 copy-done.3
  8.1 0.7 %copy.14.routes_ref = s32[64,4]{1,0:T(8,128)} copy(s32[64,4]{0,1:T(4,128)S(1)} %copy-done.3) | data formatting | bytes 2048 | tf_op args[9]
  8.8 55.8 %shard_map.127 = bf16[16,2880]{1,0:T(8,128)(2,1)} custom-call(bf16[4,16,2880]{2,1,0:T(8,128)(2,1)} %bitcast.24, bf16[64,2880]{1,0:T(8,128)(2,1)} %hidden_ref.1, bf16[8,2880]{1,0:T(8,128)(2,1)} %bitcast.25, s32[64,4]{1,0:T(8,128)} %copy.14.routes_ref, bf16[1,2880,384]{2,1,0:T(8,128)(2,1)} %gate_hbm.1, bf16[1,2880,384]{2,1,0:T(8,128)(2,1)} %up_hbm.1, ...), custom_call_target="tpu_custom_call" | custom-call | tf_op jit(solution)/shard_map/pallas_call | solution.py:326
  64.6 1.5 %copy.16 = bf16[16,2880]{1,0:T(8,128)(2,1)} copy(bf16[16,2880]{1,0:T(8,128)(2,1)} %shard_map.127) | data formatting | bytes 184320
  (5 shorter events, 0.0 us)
Async XLA Ops:
  0.0 3.6 %copy-start.2 = (bf16[64,64]{1,0:T(8,128)(2,1)S(1)}, bf16[64,64]{1,0:T(8,128)(2,1)}, u32[]{:S(2)}) copy-start(bf16[64,64]{1,0:T(8,128)(2,1)} %param.15) | copy-start | bytes 24580
  1.7 2.8 %copy-start.4 = (bf16[8,1,64,1024]{3,2,1,0:T(8,128)(2,1)S(1)}, bf16[8,1,64,1024]{3,2,1,0:T(8,128)(2,1)}, u32[]{:S(2)}) copy-start(bf16[8,1,64,1024]{3,2,1,0:T(8,128)(2,1)} %param.18) | copy-start | bytes 3145732
  4.5 0.8 %copy-start.1 = (bf16[64,64]{1,0:T(8,128)(2,1)S(1)}, bf16[64,64]{1,0:T(8,128)(2,1)}, u32[]{:S(2)}) copy-start(bf16[64,64]{1,0:T(8,128)(2,1)} %param.16) | copy-start | bytes 24580
  4.5 1.8 %copy-start = (bf16[512,2880]{0,1:T(8,128)(2,1)S(1)}, bf16[512,2880]{0,1:T(8,128)(2,1)}, u32[]{:S(2)}) copy-start(bf16[512,2880]{0,1:T(8,128)(2,1)} %param.20) | copy-start | bytes 8847364
  5.3 2.8 %copy-start.3 = (s32[64,4]{0,1:T(4,128)S(1)}, s32[64,4]{0,1:T(4,128)}, u32[]{:S(2)}) copy-start(s32[64,4]{0,1:T(4,128)} %param.22) | copy-start | bytes 3076
